TPU v7x, 32 devices: a whole 2x2x4 slice. The times are simulated.
32 devices in a mesh: sa: 4 (over y, core), sb: 8 (over z, x).
Axes of the slice: x: 2, y: 2, z: 4, core: 2. Of those that a mesh axis runs over, the one named last changes fastest.
Arguments:
- queries: bfloat16 [1024, 1024], P(('sa', 'sb')), may hold values from -6 to 6
- out_grad: bfloat16 [1024, 1024], P(('sa', 'sb')), may hold values from -6144 to 6144
- forward_out: bfloat16 [1024, 1024], P(('sa', 'sb')), may hold values from -3 to 3
- lse_shift: float32 [1024, 8], P(('sa', 'sb')), may hold values from 0.2 to 1
- key_rows: bfloat16 [32768, 256], P(('sa', 'sb')), may hold values from -7 to 7
- value_rows: bfloat16 [32768, 256], P(('sa', 'sb')), may hold values from -6 to 6
Outputs:
- query_grad: float32 [1024, 1024], P(('sa', 'sb'))
- key_grad: bfloat16 [32768, 256], P(('sa', 'sb'))
- value_grad: bfloat16 [32768, 256], P(('sa', 'sb'))
All inputs are finite; a program needn't handle non-finite values.
Results may differ from a plain program's by a relative error of at most 0.0097.
Values may be sent and summed in bfloat16 or wider, within the bound.
A program may use at most 64 MiB of HBM per device.

v0:
```python
import math

import jax
import jax.numpy as jnp
from jax import lax
from jax.sharding import PartitionSpec as P

QH = 8
KVH = 2
HEAD_DIM = 128


def head_delta(grad_part, output_part):
    product = grad_part.astype(jnp.float32) * output_part.astype(jnp.float32)
    return jnp.sum(product.reshape(product.shape[0], QH, HEAD_DIM), axis=-1)


def local(queries, out_grad, forward_out, lse_shift, key_rows, value_rows):
    per_group = QH // KVH
    score_scale = 1.0 / math.sqrt(HEAD_DIM)
    devices = lax.axis_size("sa") * lax.axis_size("sb")
    local_keys = key_rows.shape[0]
    total_keys = local_keys * devices
    key_total = lax.psum(jnp.sum(key_rows.astype(jnp.float32), axis=0), ("sa", "sb"))
    smoothed = (key_rows.astype(jnp.float32) - key_total / total_keys).astype(jnp.bfloat16)
    query_all, grad_all, output_all = (
        lax.all_gather(queries, ("sa", "sb"), axis=0, tiled=True),
        lax.all_gather(out_grad, ("sa", "sb"), axis=0, tiled=True),
        lax.all_gather(forward_out, ("sa", "sb"), axis=0, tiled=True),
    )
    shift_all = lax.all_gather(lse_shift, ("sa", "sb"), axis=0, tiled=True)
    delta_all = head_delta(grad_all, output_all)
    offset_all = shift_all + math.log(total_keys)

    def one_head(head):
        shared = head // per_group
        head_queries = lax.dynamic_slice_in_dim(query_all, head * HEAD_DIM, HEAD_DIM, 1)
        head_grads = lax.dynamic_slice_in_dim(grad_all, head * HEAD_DIM, HEAD_DIM, 1)
        head_keys = lax.dynamic_slice_in_dim(smoothed, shared * HEAD_DIM, HEAD_DIM, 1)
        head_values = lax.dynamic_slice_in_dim(value_rows, shared * HEAD_DIM, HEAD_DIM, 1)
        head_offset = lax.dynamic_slice_in_dim(offset_all, head, 1, 1)
        head_deltas = lax.dynamic_slice_in_dim(delta_all, head, 1, 1)
        scores = (
            jnp.einsum("qd,kd->qk", head_queries, head_keys, preferred_element_type=jnp.float32)
            * score_scale
        )
        prob = jnp.exp(scores - head_offset)
        prob_low = prob.astype(jnp.bfloat16)
        value_part = jnp.einsum(
            "qk,qd->kd", prob_low, head_grads, preferred_element_type=jnp.float32
        )
        dprob = jnp.einsum("qd,kd->qk", head_grads, head_values, preferred_element_type=jnp.float32)
        dscore = (prob * (dprob - head_deltas)).astype(jnp.bfloat16)
        key_part = (
            jnp.einsum("qk,qd->kd", dscore, head_queries, preferred_element_type=jnp.float32)
            * score_scale
        )
        query_part = (
            jnp.einsum("qk,kd->qd", dscore, head_keys, preferred_element_type=jnp.float32)
            * score_scale
        )
        return (query_part, key_part, value_part)

    query_heads, key_heads, value_heads = lax.map(one_head, jnp.arange(QH, dtype=jnp.int32))
    key_sum = key_heads.reshape(KVH, per_group, local_keys, HEAD_DIM).sum(axis=1)
    value_sum = value_heads.reshape(KVH, per_group, local_keys, HEAD_DIM).sum(axis=1)
    key_grad = key_sum.transpose(1, 0, 2).reshape(local_keys, KVH * HEAD_DIM).astype(jnp.bfloat16)
    value_grad = (
        value_sum.transpose(1, 0, 2).reshape(local_keys, KVH * HEAD_DIM).astype(jnp.bfloat16)
    )
    halfway = lax.psum_scatter(
        query_heads.astype(jnp.bfloat16), "sa", scatter_dimension=1, tiled=True
    )
    owned = lax.psum_scatter(halfway, "sb", scatter_dimension=1, tiled=True).astype(jnp.float32)
    query_grad = owned.transpose(1, 0, 2).reshape(owned.shape[1], QH * HEAD_DIM)
    return (query_grad, key_grad, value_grad)


def solution(mesh):
    in_specs = (
        P(("sa", "sb"), None),
        P(("sa", "sb"), None),
        P(("sa", "sb"), None),
        P(("sa", "sb"), None),
        P(("sa", "sb"), None),
        P(("sa", "sb"), None),
    )
    out_specs = (P(("sa", "sb"), None), P(("sa", "sb"), None), P(("sa", "sb"), None))
    return jax.shard_map(local, mesh=mesh, in_specs=in_specs, out_specs=out_specs, check_vma=False)
```

profile of v0, /device:TPU:0, one launch (start us, length us, event | category | flops | bytes accessed | tf_op | source)
XLA Modules:
  0.0 444.5 jit_solution(709339691636741124)
XLA Ops:
  9.5 70.8 %all-gather = f32[32,32,8]{1,2,0:T(8,128)S(1)} all-gather(f32[1,32,8]{1,2,0:T(8,128)} %bitcast.65), channel_id=1, replica_groups=mesh['sa'=4,'sb'=8] {'sa','sb'}, dimensions={0}, use_global_device_ids=true | all-gather | bytes 33792 | tf_op jit(solution)/shard_map/all_gather | solution.py:31
  81.6 37.2 %psum.7 = f32[256]{0:T(256)S(1)} all-reduce(f32[256]{0:T(256)S(1)} %convert_reduce_fusion), channel_id=1, replica_groups=mesh['sa'=4,'sb'=8] {'sa','sb'}, use_global_device_ids=true, to_apply=%region_1.0 | all-reduce | flops 256 | bytes 2048 | tf_op jit(solution)/shard_map/psum | solution.py:24
  120.0 9.0 %all-gather.9.cloned.1.call-done = bf16[1024,1024]{1,0:T(8,128)(2,1)} async-done(((bf16[32,1024]{1,0:T(8,128)(2,1)}), bf16[1024,1024]{1,0:T(8,128)(2,1)}) %all-gather.9.cloned.1.call-update) | async-done | bytes 2097168 | tf_op jit(solution)/shard_map/all_gather | solution.py:29
  128.9 3.1 multiply_bitcast_fusion
  132.1 3.0 copy.21
  135.0 3.4 reduce_sum.37
  138.6 48.5 %all-gather.5.cloned.1.call-done = bf16[1024,1024]{1,0:T(8,128)(2,1)} async-done(((bf16[32,1024]{1,0:T(8,128)(2,1)}), bf16[1024,1024]{1,0:T(8,128)(2,1)}) %all-gather.5.cloned.1.call-update) | async-done | bytes 2097168 | tf_op jit(solution)/shard_map/all_gather | solution.py:27
  187.2 152.8 %while.16 = (s32[]{:T(128)}, bf16[8,1024,128]{2,1,0:T(8,128)(2,1)}, f32[8,1024,128]{2,1,0:T(8,128)}, f32[8,1024,128]{2,1,0:T(8,128)}, s32[8]{0:T(128)S(1)}, /*in...) while((s32[]{:T(128)}, bf16[8,1024,128]{2,1,0:T(8,128)(2,1)}, ...), condition=%wide.region_4.5_spmd, body=%wide.region_3.4_spmd.sunk | while | flops 1350828032 | bytes 39090184 | solution.py:64
  191.0 3.6 fusion.56
  196.0 3.5 multiply_convert_fusion.2
  210.1 3.6 fusion.56
  215.0 3.5 multiply_convert_fusion.2
  221.0 2.9 fusion.59
  229.2 3.6 fusion.56
  234.1 3.5 multiply_convert_fusion.2
  248.3 3.6 fusion.56
  253.2 3.5 multiply_convert_fusion.2
  259.2 2.9 fusion.59
  267.4 3.6 fusion.56
  272.4 3.5 multiply_convert_fusion.2
  278.3 2.9 fusion.59
  286.5 3.6 fusion.56
  291.5 3.5 multiply_convert_fusion.2
  297.5 2.9 fusion.59
  305.6 3.6 fusion.56
  310.6 3.5 multiply_convert_fusion.2
  324.7 3.6 fusion.56
  329.7 3.5 multiply_convert_fusion.2
  335.7 2.9 fusion.59
  340.1 30.1 %reduce-scatter.3.cloned.1.call-done = bf16[8,256,128]{2,1,0:T(8,128)(2,1)} async-done(((bf16[8,1024,128]{2,1,0:T(8,128)(2,1)}), bf16[8,256,128]{2,1,0:T(8,128)(2,1)}) %reduce-scatter.3.cloned.1.call-update) | async-done | bytes 524304 | tf_op jit(solution)/shard_map/reduce_scatter | solution.py:71
  370.2 4.3 bitcast_reduce_fusion
  377.0 59.4 %reduce-scatter.5.cloned.1.call-done = bf16[8,32,128]{2,1,0:T(8,128)(2,1)} async-done(((bf16[8,256,128]{2,1,0:T(8,128)(2,1)}), bf16[8,32,128]{2,1,0:T(8,128)(2,1)}) %reduce-scatter.5.cloned.1.call-update) | async-done | bytes 65552 | tf_op jit(solution)/shard_map/reduce_scatter | solution.py:74
  (80 shorter events, 53.8 us)
Async XLA Ops:
  7.2 112.8 %all-gather.7.cloned.1.call-start = ((), (), s32[]{:S(2)}) async-start(), calls=%async_computation.3 | async-start | bytes 2162688 | tf_op jit(solution)/shard_map/all_gather | solution.py:28
  7.9 121.0 %all-gather.9.cloned.1.call-start = ((), (), s32[]{:S(2)}) async-start(), calls=%async_computation.4 | async-start | bytes 2162688 | tf_op jit(solution)/shard_map/all_gather | solution.py:29
  8.6 178.5 %all-gather.5.cloned.1.call-start = ((), (), s32[]{:S(2)}) async-start(), calls=%async_computation.2 | async-start | bytes 2162688 | tf_op jit(solution)/shard_map/all_gather | solution.py:27
  9.4 360.8 %reduce-scatter.3.cloned.1.call-start = ((), (), s32[]{:S(2)}) async-start(), calls=%async_computation.5 | async-start | bytes 2621440 | tf_op jit(solution)/shard_map/reduce_scatter | solution.py:71
  135.0 52.1 %copy-start.1 = (bf16[1024,256]{1,0:T(8,128)(2,1)S(1)}, bf16[1024,256]{1,0:T(8,128)(2,1)}, u32[]{:S(2)}) copy-start(bf16[1024,256]{1,0:T(8,128)(2,1)} %param.13) | copy-start | bytes 1572868
  196.0 6.0 %copy-start = (f32[1024,1024]{1,0:T(8,128)S(1)}, f32[1024,1024]{1,0:T(8,128)}, u32[]{:S(2)}) copy-start(f32[1024,1024]{1,0:T(8,128)} %fusion.56) | copy-start | bytes 12582916 | tf_op jit(solution)/shard_map/while
  215.0 6.0 %copy-start = (f32[1024,1024]{1,0:T(8,128)S(1)}, f32[1024,1024]{1,0:T(8,128)}, u32[]{:S(2)}) copy-start(f32[1024,1024]{1,0:T(8,128)} %fusion.56) | copy-start | bytes 12582916 | tf_op jit(solution)/shard_map/while
  234.1 6.0 %copy-start = (f32[1024,1024]{1,0:T(8,128)S(1)}, f32[1024,1024]{1,0:T(8,128)}, u32[]{:S(2)}) copy-start(f32[1024,1024]{1,0:T(8,128)} %fusion.56) | copy-start | bytes 12582916 | tf_op jit(solution)/shard_map/while
  253.2 6.0 %copy-start = (f32[1024,1024]{1,0:T(8,128)S(1)}, f32[1024,1024]{1,0:T(8,128)}, u32[]{:S(2)}) copy-start(f32[1024,1024]{1,0:T(8,128)} %fusion.56) | copy-start | bytes 12582916 | tf_op jit(solution)/shard_map/while
  272.4 6.0 %copy-start = (f32[1024,1024]{1,0:T(8,128)S(1)}, f32[1024,1024]{1,0:T(8,128)}, u32[]{:S(2)}) copy-start(f32[1024,1024]{1,0:T(8,128)} %fusion.56) | copy-start | bytes 12582916 | tf_op jit(solution)/shard_map/while
  291.5 6.0 %copy-start = (f32[1024,1024]{1,0:T(8,128)S(1)}, f32[1024,1024]{1,0:T(8,128)}, u32[]{:S(2)}) copy-start(f32[1024,1024]{1,0:T(8,128)} %fusion.56) | copy-start | bytes 12582916 | tf_op jit(solution)/shard_map/while
  310.6 6.0 %copy-start = (f32[1024,1024]{1,0:T(8,128)S(1)}, f32[1024,1024]{1,0:T(8,128)}, u32[]{:S(2)}) copy-start(f32[1024,1024]{1,0:T(8,128)} %fusion.56) | copy-start | bytes 12582916 | tf_op jit(solution)/shard_map/while
  329.7 6.0 %copy-start = (f32[1024,1024]{1,0:T(8,128)S(1)}, f32[1024,1024]{1,0:T(8,128)}, u32[]{:S(2)}) copy-start(f32[1024,1024]{1,0:T(8,128)} %fusion.56) | copy-start | bytes 12582916 | tf_op jit(solution)/shard_map/while
  340.0 96.4 %reduce-scatter.5.cloned.1.call-start = ((), (), s32[]{:S(2)}) async-start(), calls=%async_computation.6 | async-start | bytes 589824 | tf_op jit(solution)/shard_map/reduce_scatter | solution.py:74
Sparse Core Ops, SparseCore 0:
  11.0 59.4 all-gather.6
  73.4 55.4 all-gather.8
  131.9 55.1 all-gather.4
  340.1 30.0 reduce-scatter.2
  373.4 63.0 reduce-scatter.4
where the time goes:
time: 446 us; the launch traced here: 444 us
  waiting for transfers between devices  149 us (33%)
  matrix products  111 us (25%)
  blocking collectives  108 us (24%)
  loops' own time  36.7 us (8%)
  other arithmetic  14.7 us (3%)
  between operations  13.9 us (3%)
  local copies, waits for them, and re-layouts  10.5 us (2%)
    all_gather x1, blocking collectives, local(): shift_all = lax.all_gather(lse_shift, ('sa', 'sb'), axis=0, tiled=True)  70.8 us
    reduce_scatter x1, waiting for transfers between devices, local(): lax.psum_scatter(halfway, 'sb', scatter_dimension=1, tiled=True)  59.4 us
    all_gather x1, waiting for transfers between devices, local(): lax.all_gather(queries, ('sa', 'sb'), axis=0, tiled=True)  48.5 us
    psum x1, blocking collectives, local(): lax.psum(jnp.sum(key_rows.astype(jnp.float32), axis=0), ('sa', 'sb'))  37.2 us
    another operation x1, loops' own time, local(): lax.map(one_head, jnp.arange(QH, dtype=jnp.int32))  36.7 us
    reduce_scatter x1, waiting for transfers between devices, local(): lax.psum_scatter(query_heads.astype(jnp.bfloat16), 'sa', scatter_dimensio...  30.1 us
    dot_general x8, matrix products, one_head(): jnp.einsum('qd,kd->qk', head_queries, head_keys, preferred_element_type=j...  29.1 us
    dot_general x8, matrix products, one_head(): jnp.einsum('qd,kd->qk', head_grads, head_values, preferred_element_type=j...  27.7 us
  transfers between devices with their start and end apart: 5, of which 4 were waited for; matrix products, arithmetic and copies ran while one was open for 4% of the time, Pallas kernels for 0%

commit v1 on v0

v1 whole, which is shorter than its diff:
```python
import functools
import math

import jax
import jax.numpy as jnp
from jax import lax
from jax.experimental import pallas as pl
from jax.experimental.pallas import tpu as pltpu
from jax.sharding import PartitionSpec as P

QH = 8
KVH = 2
HEAD_DIM = 128
MESH = pl.DeviceIdType.MESH
BF = jnp.bfloat16
F32 = jnp.float32
AXES = ("sa", "sb")


def grid_of(sa, sb):
    inner = 2 ** (int(math.log2(sb)) // 2)
    return sa // 2, sb // inner, inner


class Place:
    def __init__(self, dims):
        self.dims = dims
        sa, sb = lax.axis_index("sa"), lax.axis_index("sb")
        self.core = sa % 2
        self.at = (sa // 2, sb // dims[2], sb % dims[2])

    def other(self, axis, step):
        at = list(self.at)
        at[axis] = (at[axis] + step) % self.dims[axis]
        return tuple(at)

    def back(self, offset):
        return tuple((p + n - o) % n for p, n, o in zip(self.at, self.dims, offset))

    def device(self, at):
        return (at[0] * 2 + self.core, at[1] * self.dims[2] + at[2])

    def partner(self):
        return (self.at[0] * 2 + 1 - self.core, lax.axis_index("sb"))

    def slot(self, at):
        return (at[0] * self.dims[1] + at[1]) * self.dims[2] + at[2]

    def greet(self):
        barrier = pltpu.get_barrier_semaphore()
        peers = [self.partner()]
        for axis in range(3):
            for step in range(1, self.dims[axis]):
                peers.append(self.device(self.other(axis, step)))
        for peer in peers:
            pl.semaphore_signal(barrier, inc=1, device_id=peer, device_id_type=MESH)
        pl.semaphore_wait(barrier, len(peers))


def pieces(x):
    hi = x.astype(BF)
    rest = x - hi.astype(F32)
    mid = rest.astype(BF)
    low = (rest - mid.astype(F32)).astype(BF)
    return hi, mid, low


def gather_sends(dims):
    na, nb, nd = dims
    sends = []
    for step in range(1, nb):
        sends.append(("qdx", (0, 0, 0), 1, step))
    for step in range(1, nd):
        sends.append(("qdx", (0, 0, 0), 2, step))
    for step in range(1, na):
        sends.append(("qdx", (0, 0, 0), 0, step))
    for b in range(1, nb):
        for step in range(1, nd):
            sends.append(("qdx", (0, b, 0), 2, step))
        for step in range(1, na):
            sends.append(("qdx", (0, b, 0), 0, step))
    for b in range(nb):
        for d in range(1, nd):
            for step in range(1, na):
                sends.append(("qx", (0, b, d), 0, step))
        for a in range(1, na):
            for step in range(1, nd):
                sends.append(("d", (a, b, 0), 2, step))
    return sends


def gather_kernel(dims, total_keys, q_ref, d_ref, o_ref, lse_ref, k_ref, v_ref,
                  qa_ref, da_ref, aux_ref, ks_ref, va_ref,
                  xa, kraw, half, halfr, send_sem, q_sem, d_sem, x_sem, kv_send, kv_recv):
    place = Place(dims)
    rows = q_ref.shape[0]
    keys = k_ref.shape[0]
    me = place.slot(place.at)
    scale = 1.0 / math.sqrt(HEAD_DIM)
    place.greet()

    def to_partner(src, dst, n):
        copy = pltpu.make_async_remote_copy(
            src_ref=src, dst_ref=dst, send_sem=kv_send.at[n], recv_sem=kv_recv.at[n],
            device_id=place.partner(), device_id_type=MESH)
        copy.start()
        return copy

    partner_copies = [to_partner(k_ref, kraw, 0), to_partner(v_ref, va_ref.at[1], 1)]

    bufs = {"q": (qa_ref, q_sem), "d": (da_ref, d_sem), "x": (xa, x_sem)}
    own = {"q": q_ref, "d": d_ref}
    started = []

    def flat(offset):
        return (offset[0] * dims[1] + offset[1]) * dims[2] + offset[2]

    def send(kind, offset, axis, step):
        buf, sem = bufs[kind]
        slot = place.slot(place.back(offset))
        src = own[kind] if kind in own and offset == (0, 0, 0) else buf.at[slot]
        there = list(offset)
        there[axis] = (there[axis] + step) % dims[axis]
        copy = pltpu.make_async_remote_copy(
            src_ref=src, dst_ref=buf.at[slot],
            send_sem=send_sem.at[len(started)], recv_sem=sem.at[flat(there)],
            device_id=place.device(place.other(axis, step)), device_id_type=MESH)
        copy.start()
        started.append(copy)

    arrived = set()

    def need(kind, offset):
        if offset == (0, 0, 0) or (kind, offset) in arrived:
            return
        arrived.add((kind, offset))
        buf, sem = bufs[kind]
        slot = place.slot(place.back(offset))
        pltpu.make_async_remote_copy(
            src_ref=buf.at[slot], dst_ref=buf.at[slot],
            send_sem=send_sem.at[0], recv_sem=sem.at[flat(offset)],
            device_id=place.partner(), device_id_type=MESH).wait_recv()

    sends = gather_sends(dims)
    first = [s for s in sends if s[1] == (0, 0, 0)]
    for kind in "qd":
        for kinds, offset, axis, step in first:
            if kind in kinds:
                send(kind, offset, axis, step)

    lane = lax.broadcasted_iota(jnp.int32, (rows, HEAD_DIM), 1)
    aux = jnp.zeros((rows, HEAD_DIM), F32)
    for head in range(QH):
        cols = pl.ds(head * HEAD_DIM, HEAD_DIM)
        product = d_ref[:, cols].astype(F32) * o_ref[:, cols].astype(F32)
        delta = jnp.sum(product, axis=1, keepdims=True)
        offset = (lse_ref[:, head:head + 1] + math.log(total_keys)) * (1.0 / scale)
        for at, value in ((0, offset), (3 * QH, delta)):
            for n, piece in enumerate(pieces(value)):
                aux = jnp.where(lane == at + 3 * head + n, piece.astype(F32), aux)
    xa[me, pl.ds(0, rows), :] = aux.astype(BF)
    chunk = 128

    def add_rows(n, acc):
        block = k_ref[pl.ds(pl.multiple_of(n * chunk, chunk), chunk), :].astype(F32)
        return acc + jnp.sum(block, axis=0, keepdims=True)

    key_sum = lax.fori_loop(0, keys // chunk, add_rows, jnp.zeros((1, KVH * HEAD_DIM), F32))
    row = lax.broadcasted_iota(jnp.int32, (16, HEAD_DIM), 0)
    small = jnp.zeros((16, HEAD_DIM), F32)
    for n, piece in enumerate(pieces(key_sum)):
        for c in range(KVH):
            part = piece[:, c * HEAD_DIM:(c + 1) * HEAD_DIM].astype(F32)
            small = jnp.where(row == 2 * n + c, part, small)
    xa[me, pl.ds(rows, 16), :] = small.astype(BF)
    for kinds, offset, axis, step in first:
        send("x", offset, axis, step)

    qa_ref[me] = q_ref[...]
    da_ref[me] = d_ref[...]
    va_ref[0] = v_ref[...]
    for kinds, offset, axis, step in sends:
        if offset == (0, 0, 0):
            continue
        for kind in kinds:
            need(kind, offset)
            send(kind, offset, axis, step)
    for a in range(dims[0]):
        for b in range(dims[1]):
            for d in range(dims[2]):
                for kind in "qdx":
                    need(kind, (a, b, d))

    members = dims[0] * dims[1] * dims[2]
    half_sum = jnp.zeros((16, HEAD_DIM), F32)
    for g in range(members):
        half_sum = half_sum + xa[g, pl.ds(rows, 16), :].astype(F32)
        aux_ref[pl.ds(g * rows, rows), :] = xa[g, pl.ds(0, rows), :]
    half[...] = half_sum
    partner_copies.append(to_partner(half, halfr, 2))
    for copy in partner_copies:
        copy.wait()
    both = half[...] + halfr[...]
    for c in range(KVH):
        cols = pl.ds(c * HEAD_DIM, HEAD_DIM)
        mean = (both[c:c + 1] + both[c + 2:c + 3] + both[c + 4:c + 5]) / total_keys

        def smooth(n, carry):
            at = pl.ds(pl.multiple_of(n * chunk, chunk), chunk)
            ks_ref[0, at, cols] = (k_ref[at, cols].astype(F32) - mean).astype(BF)
            ks_ref[1, at, cols] = (kraw[at, cols].astype(F32) - mean).astype(BF)
            return carry

        lax.fori_loop(0, keys // chunk, smooth, 0)
    for copy in started:
        copy.wait_send()


def gather(dims, total_keys, q, d, o, lse, k, v):
    members = dims[0] * dims[1] * dims[2]
    rows, width = q.shape
    keys, kw = k.shape
    count = sum(len(s[0]) for s in gather_sends(dims))
    vmem = pl.BlockSpec(memory_space=pltpu.VMEM)
    return pl.pallas_call(
        functools.partial(gather_kernel, dims, total_keys),
        name="gather",
        out_shape=(
            jax.ShapeDtypeStruct((members, rows, width), BF),
            jax.ShapeDtypeStruct((members, rows, width), BF),
            jax.ShapeDtypeStruct((members * rows, HEAD_DIM), BF),
            jax.ShapeDtypeStruct((2, keys, kw), BF),
            jax.ShapeDtypeStruct((2, keys, kw), BF),
        ),
        in_specs=[vmem] * 6,
        out_specs=(vmem,) * 5,
        scratch_shapes=[
            pltpu.VMEM((members, rows + 16, HEAD_DIM), BF),
            pltpu.VMEM((keys, kw), BF),
            pltpu.VMEM((16, HEAD_DIM), F32),
            pltpu.VMEM((16, HEAD_DIM), F32),
            pltpu.SemaphoreType.DMA((count,)),
            pltpu.SemaphoreType.DMA((members,)),
            pltpu.SemaphoreType.DMA((members,)),
            pltpu.SemaphoreType.DMA((members,)),
            pltpu.SemaphoreType.DMA((3,)),
            pltpu.SemaphoreType.DMA((3,)),
        ],
        compiler_params=pltpu.CompilerParams(collective_id=0, has_side_effects=True),
    )(q, d, o, lse, k, v)


def attend_kernel(q_ref, d_ref, aux_ref, k_ref, v_ref, dq_ref, dk_ref, dv_ref, acc):
    c, tile = pl.program_id(0), pl.program_id(1)
    per_group = QH // KVH
    scale = 1.0 / math.sqrt(HEAD_DIM)
    keys = k_ref[...]
    values = v_ref[...]
    aux = aux_ref[...]
    lane = lax.broadcasted_iota(jnp.int32, keys.shape, 1)
    nt = (((1,), (1,)), ((), ()))
    dk = jnp.zeros(keys.shape, F32)
    dv = jnp.zeros(keys.shape, F32)
    for g in range(per_group):
        head = c * per_group + g
        cols = pl.ds(g * HEAD_DIM, HEAD_DIM)
        heads_q = q_ref[:, cols]
        heads_d = d_ref[:, cols]
        at = 3 * head
        minus_s = jnp.where((lane >= at) & (lane < at + 3), -1.0, 0.0).astype(BF)
        at = 3 * QH + 3 * head
        minus_d = jnp.where((lane >= at) & (lane < at + 3), -1.0, 0.0).astype(BF)
        s = lax.dot_general(jnp.concatenate([keys, minus_s], 1),
                            jnp.concatenate([heads_q, aux], 1), nt,
                            preferred_element_type=F32)
        dp = lax.dot_general(jnp.concatenate([values, minus_d], 1),
                             jnp.concatenate([heads_d, aux], 1), nt,
                             preferred_element_type=F32)
        prob = jnp.exp2(s * (scale * math.log2(math.e)))
        dv = dv + jnp.dot(prob.astype(BF), heads_d, preferred_element_type=F32)
        ds = (prob * dp).astype(BF)
        dk = dk + jnp.dot(ds, heads_q, preferred_element_type=F32)
        dq = lax.dot_general(ds, keys, (((0,), (0,)), ((), ())), preferred_element_type=F32)

        @pl.when(tile == 0)
        def _():
            acc[:, cols] = dq

        @pl.when(tile > 0)
        def _():
            acc[:, cols] += dq

    dk_ref[...] = (dk * scale).astype(BF)
    dv_ref[...] = dv.astype(BF)

    @pl.when(tile == pl.num_programs(1) - 1)
    def _():
        dq_ref[...] = (acc[...] * scale).astype(BF)


def attend(q, d, aux, k, v, tile=512):
    rows, width = q.shape
    keys, kw = k.shape
    tile = min(tile, keys)
    group = width // KVH
    key_spec = pl.BlockSpec((tile, HEAD_DIM), lambda c, t: (t, c))
    row_spec = pl.BlockSpec((rows, group), lambda c, t: (0, c))
    return pl.pallas_call(
        attend_kernel,
        name="attend",
        grid=(KVH, keys // tile),
        out_shape=(
            jax.ShapeDtypeStruct((rows, width), BF),
            jax.ShapeDtypeStruct((keys, kw), BF),
            jax.ShapeDtypeStruct((keys, kw), BF),
        ),
        in_specs=[row_spec, row_spec, pl.BlockSpec((rows, HEAD_DIM), lambda c, t: (0, 0)),
                  key_spec, key_spec],
        out_specs=(row_spec, key_spec, key_spec),
        scratch_shapes=[pltpu.VMEM((rows, group), F32)],
        compiler_params=pltpu.CompilerParams(dimension_semantics=("arbitrary", "arbitrary")),
    )(q, d, aux, k, v)


def reduce_kernel(dims, p_ref, dk_ref, dv_ref, dq_out, dk_out, dv_out,
                  kvr, r1a, r1b, t1a, t1b, r2a, r2b, t2, r3, send_sem, recv_sem):
    na, nb, nd = dims
    place = Place(dims)
    a, b, d = place.at
    half = p_ref.shape[-1] // 2
    left, right = pl.ds(0, half), pl.ds(half, half)
    place.greet()
    copies = []

    def send(src, dst, device):
        n = len(copies)
        copy = pltpu.make_async_remote_copy(
            src_ref=src, dst_ref=dst, send_sem=send_sem.at[n], recv_sem=recv_sem.at[n],
            device_id=device, device_id_type=MESH)
        copy.start()
        copies.append(copy)
        return copy

    stage = []
    for s in range(1, nd):
        to = place.other(2, s)
        stage.append(send(p_ref.at[:, :, to[2], :, left], r1a.at[s - 1], place.device(to)))
    for s in range(1, na):
        to = place.other(0, s)
        stage.append(send(p_ref.at[to[0], :, :, :, right], r1b.at[s - 1], place.device(to)))
    kv = [send(dk_ref.at[1], kvr.at[0], place.partner()),
          send(dv_ref.at[1], kvr.at[1], place.partner())]
    for copy in stage:
        copy.wait_recv()

    for i in range(na):
        for j in range(nb):
            total = p_ref[i, j, d, :, left].astype(F32)
            for s in range(nd - 1):
                total = total + r1a[s, i, j].astype(F32)
            t1a[i, j] = total.astype(BF)
    for j in range(nb):
        for i in range(nd):
            total = p_ref[a, j, i, :, right].astype(F32)
            for s in range(na - 1):
                total = total + r1b[s, j, i].astype(F32)
            t1b[i, j] = total.astype(BF)

    stage2 = []
    for s in range(1, na):
        to = place.other(0, s)
        stage2.append(send(t1a.at[to[0]], r2a.at[s - 1], place.device(to)))
    for s in range(1, nd):
        to = place.other(2, s)
        stage2.append(send(t1b.at[to[2]], r2b.at[s - 1], place.device(to)))
    for copy in stage2:
        copy.wait_recv()
    for j in range(nb):
        total = t1a[a, j].astype(F32)
        for s in range(na - 1):
            total = total + r2a[s, j].astype(F32)
        t2[j, :, left] = total.astype(BF)
        total = t1b[d, j].astype(F32)
        for s in range(nd - 1):
            total = total + r2b[s, j].astype(F32)
        t2[j, :, right] = total.astype(BF)
    stage3 = []
    for s in range(1, nb):
        to = place.other(1, s)
        stage3.append(send(t2.at[to[1]], r3.at[s - 1], place.device(to)))

    for copy in kv:
        copy.wait_recv()
    chunk = 128

    def add_part(n, carry):
        at = pl.ds(pl.multiple_of(n * chunk, chunk), chunk)
        dk_out[at, :] = (dk_ref[0, at, :].astype(F32) + kvr[0, at, :].astype(F32)).astype(BF)
        dv_out[at, :] = (dv_ref[0, at, :].astype(F32) + kvr[1, at, :].astype(F32)).astype(BF)
        return carry

    lax.fori_loop(0, dk_out.shape[0] // chunk, add_part, 0)
    for copy in stage3:
        copy.wait_recv()
    total = t2[b].astype(F32)
    for s in range(nb - 1):
        total = total + r3[s].astype(F32)
    dq_out[...] = total
    for copy in copies:
        copy.wait_send()


def reduce(dims, partial, dk, dv):
    na, nb, nd = dims
    rows, width = partial.shape[-2:]
    half = width // 2
    keys, kw = dk.shape[1:]
    count = 2 * (na - 1) + 2 * (nd - 1) + (nb - 1) + 2
    vmem = pl.BlockSpec(memory_space=pltpu.VMEM)
    return pl.pallas_call(
        functools.partial(reduce_kernel, dims),
        name="reduce",
        out_shape=(
            jax.ShapeDtypeStruct((rows, width), F32),
            jax.ShapeDtypeStruct((keys, kw), BF),
            jax.ShapeDtypeStruct((keys, kw), BF),
        ),
        in_specs=[vmem] * 3,
        out_specs=(vmem,) * 3,
        scratch_shapes=[
            pltpu.VMEM((2, keys, kw), BF),
            pltpu.VMEM((max(nd - 1, 1), na, nb, rows, half), BF),
            pltpu.VMEM((max(na - 1, 1), nb, nd, rows, half), BF),
            pltpu.VMEM((na, nb, rows, half), BF),
            pltpu.VMEM((nd, nb, rows, half), BF),
            pltpu.VMEM((max(na - 1, 1), nb, rows, half), BF),
            pltpu.VMEM((max(nd - 1, 1), nb, rows, half), BF),
            pltpu.VMEM((nb, rows, width), BF),
            pltpu.VMEM((max(nb - 1, 1), rows, width), BF),
            pltpu.SemaphoreType.DMA((count,)),
            pltpu.SemaphoreType.DMA((count,)),
        ],
        compiler_params=pltpu.CompilerParams(collective_id=1, has_side_effects=True),
    )(partial, dk, dv)


def local(dims, queries, out_grad, forward_out, lse_shift, key_rows, value_rows):
    members = dims[0] * dims[1] * dims[2]
    rows, width = queries.shape
    keys, kw = key_rows.shape
    total_keys = keys * members * 2
    q, d, aux, k, v = gather(
        dims, total_keys, queries, out_grad, forward_out, lse_shift, key_rows, value_rows)
    dq, dk, dv = attend(
        q.reshape(members * rows, width), d.reshape(members * rows, width), aux,
        k.reshape(2 * keys, kw), v.reshape(2 * keys, kw))
    return reduce(dims, dq.reshape(*dims, rows, width),
                  dk.reshape(2, keys, kw), dv.reshape(2, keys, kw))


def solution(mesh):
    dims = grid_of(mesh.shape["sa"], mesh.shape["sb"])
    spec = P(("sa", "sb"), None)
    return jax.shard_map(functools.partial(local, dims), mesh=mesh, in_specs=(spec,) * 6,
                         out_specs=(spec,) * 3, check_vma=False)
```

time: 446 us -> 105 us (0.24)
  waiting for transfers between devices: 149 us -> 0 us
  matrix products: 111 us -> 0 us
  blocking collectives: 108 us -> 0 us
  Pallas kernels: 0 us -> 97.9 us
  loops' own time: 36.7 us -> 0 us
  other arithmetic: 14.7 us -> 0 us
  between operations: 13.9 us -> 0.65 us
  local copies, waits for them, and re-layouts: 10.5 us -> 5.66 us
    dot_general x40 -> x0, matrix products: 111 us -> none  [the longest x8 29.1 us: one_head(): jnp.einsum('qd,kd->qk', head_queries, head_keys, preferred_element_type=j...]
    pallas_call x0 -> x3, Pallas kernels: none -> 97.9 us  [the longest x1 38.9 us: gather(): pl.pallas_call(functools.partial(gather_kernel, dims, total_keys), name='...]
    reduce_scatter x2 -> x0, waiting for transfers between devices: 89.6 us -> none  [the longest x1 59.4 us: local(): lax.psum_scatter(halfway, 'sb', scatter_dimension=1, tiled=True)]
    all_gather x1 -> x0, blocking collectives: 70.8 us -> none  [local(): shift_all = lax.all_gather(lse_shift, ('sa', 'sb'), axis=0, tiled=True)]
    all_gather x3 -> x0, waiting for transfers between devices: 57.5 us -> none  [the longest x1 48.5 us: local(): lax.all_gather(queries, ('sa', 'sb'), axis=0, tiled=True)]
    psum x1 -> x0, blocking collectives: 37.2 us -> none  [local(): lax.psum(jnp.sum(key_rows.astype(jnp.float32), axis=0), ('sa', 'sb'))]
    another operation x1 -> x0, loops' own time: 36.7 us -> none  [local(): lax.map(one_head, jnp.arange(QH, dtype=jnp.int32))]
    reduce_sum x3 -> x0, other arithmetic: 8.95 us -> none  [the longest x1 4.34 us: local(): value_heads.reshape(KVH, per_group, local_keys, HEAD_DIM).sum(axis=1)]
  transfers between devices with their start and end apart: 5 -> 0, of which waited for: 4 -> 0; matrix products, arithmetic and copies ran while one was open for 4% -> 0% of each run, Pallas kernels for 0% -> 0%
where the time goes in v1:
time: 105 us; the launch traced here: 104 us
  Pallas kernels  97.9 us (93%)
  local copies, waits for them, and re-layouts  5.66 us (5%)
    pallas_call x1, Pallas kernels, gather(): pl.pallas_call(functools.partial(gather_kernel, dims, total_keys), name='...  38.9 us
    pallas_call x1, Pallas kernels, attend(): pl.pallas_call(attend_kernel, name='attend', grid=(KVH, keys // tile), ou...  34.9 us
    pallas_call x1, Pallas kernels, reduce(): pl.pallas_call(functools.partial(reduce_kernel, dims), name='reduce', out...  24.1 us
    unnamed x6, local copies, waits for them, and re-layouts  5.66 us

profile of v1, /device:TPU:0, one launch (start us, length us, event | category | flops | bytes accessed | tf_op | source)
XLA Modules:
  0.0 104.3 jit_solution(7449710842656934565)
XLA Ops:
  0.6 1.4 %copy.9.lse_ref = f32[32,8]{1,0:T(8,128)} copy(f32[32,8]{0,1:T(8,128)} %param.9) | data formatting | bytes 2048 | tf_op args[3]
  2.0 38.9 %gather.1 = (bf16[16,32,1024]{2,1,0:T(8,128)(2,1)}, bf16[16,32,1024]{2,1,0:T(8,128)(2,1)}, bf16[512,128]{1,0:T(8,128)(2,1)}, bf16[2,1024,256]{2,1,0:T(8,128)(2,1)}, bf16[2,1024,256]{2,1,0:T(8,128)(2,1)}) custom-call(bf16[32,1024]{1,0:T(8,128)(2,1)} %q_ref.1, bf16[32,1024]{1,0:T(8,128)(2,1)} %d_ref.1, bf16[32,1024]{1,0:T(8,128)(2,1)} %o_ref.1, ...), custom_call_target="tpu_custom_call" | custom-call | tf_op jit(solution)/shard_map/gather/pallas_call | solution.py:225
  40.9 34.9 %attend.1 = (bf16[512,1024]{1,0:T(8,128)(2,1)}, bf16[2048,256]{1,0:T(8,128)(2,1)}, bf16[2048,256]{1,0:T(8,128)(2,1)}) custom-call(bf16[512,1024]{1,0:T(8,128)(2,1)} %bitcast.10, bf16[512,1024]{1,0:T(8,128)(2,1)} %bitcast.11, bf16[512,128]{1,0:T(8,128)(2,1)} %get-tuple-element.13.aux_ref, bf16[2048,256]{1,0:T(8,128)(2,1)} %bitcast.12, bf16[2048,256]{1,0:T(8,128)(2,1)} %bitcast.13), custom_call_target="tpu_custom_call" | custom-call | tf_op jit(solution)/shard_map/attend/pallas_call | solution.py:308
  75.8 24.1 %reduce.1 = (f32[32,1024]{1,0:T(8,128)}, bf16[1024,256]{1,0:T(8,128)(2,1)}, bf16[1024,256]{1,0:T(8,128)(2,1)}) custom-call(bf16[2,4,2,32,1024]{4,3,2,1,0:T(8,128)(2,1)} %bitcast.7, bf16[2,1024,256]{2,1,0:T(8,128)(2,1)} %bitcast.8, bf16[2,1024,256]{2,1,0:T(8,128)(2,1)} %bitcast.9), custom_call_target="tpu_custom_call" | custom-call | tf_op jit(solution)/shard_map/reduce/pallas_call | solution.py:420
  100.0 1.6 %copy.13 = f32[32,1024]{1,0:T(8,128)} copy(f32[32,1024]{1,0:T(8,128)} %get-tuple-element.22) | data formatting | bytes 262144
  101.5 0.0 copy-start
  101.5 1.9 %copy.14 = bf16[1024,256]{1,0:T(8,128)(2,1)} copy(bf16[1024,256]{1,0:T(8,128)(2,1)} %get-tuple-element.23) | data formatting | bytes 1048576
  103.5 0.0 copy-done
  103.5 0.8 copy.15
Async XLA Ops:
  101.5 1.9 %copy-start = (bf16[1024,256]{1,0:T(8,128)(2,1)S(1)}, bf16[1024,256]{1,0:T(8,128)(2,1)}, u32[]{:S(2)}) copy-start(bf16[1024,256]{1,0:T(8,128)(2,1)} %get-tuple-element.24) | copy-start | bytes 1572868

commit v2 on v0

v2 whole, which is shorter than its diff:
```python
import functools
import math

import jax
import jax.numpy as jnp
from jax import lax
from jax.experimental import pallas as pl
from jax.experimental.pallas import tpu as pltpu
from jax.sharding import PartitionSpec as P

QH = 8
KVH = 2
HEAD_DIM = 128
MESH = pl.DeviceIdType.MESH
BF = jnp.bfloat16
F32 = jnp.float32
AXES = ("sa", "sb")


def grid_of(sa, sb):
    inner = 2 ** (int(math.log2(sb)) // 2)
    return sa // 2, sb // inner, inner


class Place:
    def __init__(self, dims):
        self.dims = dims
        sa, sb = lax.axis_index("sa"), lax.axis_index("sb")
        self.core = sa % 2
        self.at = (sa // 2, sb // dims[2], sb % dims[2])

    def other(self, axis, step):
        at = list(self.at)
        at[axis] = (at[axis] + step) % self.dims[axis]
        return tuple(at)

    def back(self, offset):
        return tuple((p + n - o) % n for p, n, o in zip(self.at, self.dims, offset))

    def device(self, at):
        return (at[0] * 2 + self.core, at[1] * self.dims[2] + at[2])

    def partner(self):
        return (self.at[0] * 2 + 1 - self.core, lax.axis_index("sb"))

    def slot(self, at):
        return (at[0] * self.dims[1] + at[1]) * self.dims[2] + at[2]

    def greet(self):
        barrier = pltpu.get_barrier_semaphore()
        peers = [self.partner()]
        for axis in range(3):
            for step in range(1, self.dims[axis]):
                peers.append(self.device(self.other(axis, step)))
        for peer in peers:
            pl.semaphore_signal(barrier, inc=1, device_id=peer, device_id_type=MESH)
        pl.semaphore_wait(barrier, len(peers))


def pieces(x):
    hi = x.astype(BF)
    rest = x - hi.astype(F32)
    mid = rest.astype(BF)
    low = (rest - mid.astype(F32)).astype(BF)
    return hi, mid, low


def relay_sends(dims):
    na, nb, nd = dims
    line, corner = [], []
    for b in range(1, nb):
        line += [((0, b, 0), 2, step) for step in range(1, nd)]
        line += [((0, b, 0), 0, step) for step in range(1, na)]
    for b in range(nb):
        corner += [("x", (0, b, d), 0, s) for d in range(1, nd) for s in range(1, na)]
        corner += [("d", (a, b, 0), 2, s) for a in range(1, na) for s in range(1, nd)]
    return line, corner


def first_sends(dims):
    along = [(1, step) for step in range(1, dims[1])]
    across = [(2, step) for step in range(1, dims[2])] + [(0, step) for step in range(1, dims[0])]
    return along, across


def counts(dims):
    na, nb, nd = dims
    line, corner = relay_sends(dims)
    along, across = first_sends(dims)
    own = len(along) + len(across) + len(line)
    x_diag = sum(1 for c in corner if c[0] == "x")
    gathered = 5 * own + 3 * x_diag + 2 * (len(corner) - x_diag)
    reduced = 2 * (2 * (na - 1) + 2 * (nd - 1) + (nb - 1))
    return gathered, reduced


def whole_kernel(dims, total_keys, tile, q_ref, d_ref, o_ref, lse_ref, k_ref, v_ref,
                 dq_out, dk_out, dv_out,
                 qa, da, xa, aux_ref, ks, va, half, halfr, acc, part, dks, dvs, kvr,
                 r1a, r1b, t1a, t1b, r2a, r2b, t2, r3,
                 send_sem, q_sem, d_sem, x_sem, kv_send, kv_recv, red_send, red_recv):
    na, nb, nd = dims
    members = na * nb * nd
    place = Place(dims)
    pa, pb, pd = place.at
    rows = q_ref.shape[0]
    keys = k_ref.shape[0]
    group = q_ref.shape[1] // KVH
    per_group = QH // KVH
    me = place.slot(place.at)
    scale = 1.0 / math.sqrt(HEAD_DIM)
    place.greet()
    line, corner = relay_sends(dims)
    along, across = first_sends(dims)
    origin = (0, 0, 0)

    partner_copies = []

    def to_partner(src, dst):
        n = len(partner_copies)
        copy = pltpu.make_async_remote_copy(
            src_ref=src, dst_ref=dst, send_sem=kv_send.at[n], recv_sem=kv_recv.at[n],
            device_id=place.partner(), device_id_type=MESH)
        copy.start()
        partner_copies.append(copy)
        return copy

    to_partner(k_ref, ks.at[1])
    to_partner(v_ref, va.at[1])

    def flat(offset):
        return (offset[0] * nb + offset[1]) * nd + offset[2]

    def places(kind, slot, offset):
        if kind == "x":
            return xa.at[slot], x_sem.at[flat(offset)]
        c = int(kind[1])
        buf, sem = (qa, q_sem) if kind[0] == "q" else (da, d_sem)
        return buf.at[c, slot], sem.at[c, flat(offset)]

    started = []

    def send(kind, offset, axis, step):
        slot = place.slot(place.back(offset))
        there = list(offset)
        there[axis] = (there[axis] + step) % dims[axis]
        ref, sem = places(kind, slot, there)
        src = ref
        if offset == origin and kind != "x":
            src = (q_ref if kind[0] == "q" else d_ref).at[:, pl.ds(int(kind[1]) * group, group)]
        copy = pltpu.make_async_remote_copy(
            src_ref=src, dst_ref=ref, send_sem=send_sem.at[len(started)], recv_sem=sem,
            device_id=place.device(place.other(axis, step)), device_id_type=MESH)
        copy.start()
        started.append(copy)

    arrived = set()

    def need(kind, offset):
        if offset == origin or (kind, offset) in arrived:
            return
        arrived.add((kind, offset))
        ref, sem = places(kind, place.slot(place.back(offset)), offset)
        pltpu.make_async_remote_copy(
            src_ref=ref, dst_ref=ref, send_sem=send_sem.at[0], recv_sem=sem,
            device_id=place.partner(), device_id_type=MESH).wait_recv()

    def send_first(kind, directions):
        for axis, step in directions:
            send(kind, origin, axis, step)

    def send_line(kinds):
        for offset, axis, step in line:
            for kind in kinds:
                need(kind, offset)
                send(kind, offset, axis, step)

    def send_corner(kinds):
        for which, offset, axis, step in corner:
            for kind in kinds:
                if (kind[0] == "d") == (which == "d"):
                    need(kind, offset)
                    send(kind, offset, axis, step)

    def need_all(kinds):
        for a in range(na):
            for b in range(nb):
                for d in range(nd):
                    for kind in kinds:
                        need(kind, (a, b, d))

    for kind in ("q0", "d0"):
        send_first(kind, along + across)

    lane = lax.broadcasted_iota(jnp.int32, (rows, HEAD_DIM), 1)
    aux = jnp.zeros((rows, HEAD_DIM), F32)
    for head in range(QH):
        cols = pl.ds(head * HEAD_DIM, HEAD_DIM)
        product = d_ref[:, cols].astype(F32) * o_ref[:, cols].astype(F32)
        delta = jnp.sum(product, axis=1, keepdims=True)
        offset = (lse_ref[:, head:head + 1] + math.log(total_keys)) * (1.0 / scale)
        for at, value in ((0, offset), (3 * QH, delta)):
            for n, piece in enumerate(pieces(value)):
                aux = jnp.where(lane == at + 3 * head + n, piece.astype(F32), aux)
    xa[me, pl.ds(0, rows), :] = aux.astype(BF)
    chunk = 128

    def add_rows(n, total):
        block = k_ref[pl.ds(pl.multiple_of(n * chunk, chunk), chunk), :].astype(F32)
        return total + jnp.sum(block, axis=0, keepdims=True)

    key_sum = lax.fori_loop(0, keys // chunk, add_rows, jnp.zeros((1, KVH * HEAD_DIM), F32))
    row = lax.broadcasted_iota(jnp.int32, (16, HEAD_DIM), 0)
    small = jnp.zeros((16, HEAD_DIM), F32)
    for n, piece in enumerate(pieces(key_sum)):
        for c in range(KVH):
            term = piece[:, c * HEAD_DIM:(c + 1) * HEAD_DIM].astype(F32)
            small = jnp.where(row == 2 * n + c, term, small)
    xa[me, pl.ds(rows, 16), :] = small.astype(BF)
    send_first("x", along + across)
    for kind in ("q1", "d1"):
        send_first(kind, along)
    for c in range(KVH):
        qa[c, me] = q_ref[:, pl.ds(c * group, group)]
        da[c, me] = d_ref[:, pl.ds(c * group, group)]
    va[0] = v_ref[...]
    send_line(("x",))
    send_line(("q0", "d0"))
    send_corner(("x",))
    send_corner(("q0", "d0"))
    for kind in ("q1", "d1"):
        send_first(kind, across)

    need_all(("x",))
    half_sum = jnp.zeros((16, HEAD_DIM), F32)
    for g in range(members):
        half_sum = half_sum + xa[g, pl.ds(rows, 16), :].astype(F32)
        aux_ref[pl.ds(g * rows, rows), :] = xa[g, pl.ds(0, rows), :]
    half[...] = half_sum
    to_partner(half, halfr)
    send_line(("q1", "d1"))
    for copy in partner_copies:
        copy.wait_recv()
    both = half[...] + halfr[...]
    for c in range(KVH):
        cols = pl.ds(c * HEAD_DIM, HEAD_DIM)
        mean = (both[c:c + 1] + both[c + 2:c + 3] + both[c + 4:c + 5]) / total_keys

        def smooth(n, carry):
            at = pl.ds(pl.multiple_of(n * chunk, chunk), chunk)
            ks[0, at, cols] = (k_ref[at, cols].astype(F32) - mean).astype(BF)
            ks[1, at, cols] = (ks[1, at, cols].astype(F32) - mean).astype(BF)
            return carry

        lax.fori_loop(0, keys // chunk, smooth, 0)
    need_all(("q0", "d0"))

    nt = (((1,), (1,)), ((), ()))
    tiles = keys // tile
    key_lane = lax.broadcasted_iota(jnp.int32, (tile, HEAD_DIM), 1)

    def attend(c, side, first):
        cols = pl.ds(c * HEAD_DIM, HEAD_DIM)

        def one(t, carry):
            at = pl.ds(pl.multiple_of(t * tile, tile), tile)
            kt = ks[side, at, cols]
            vt = va[side, at, cols]
            aux_all = aux_ref[...]
            dk = jnp.zeros((tile, HEAD_DIM), F32)
            dv = jnp.zeros((tile, HEAD_DIM), F32)
            for g in range(per_group):
                head_cols = pl.ds(g * HEAD_DIM, HEAD_DIM)
                heads_q = qa[c, :, :, head_cols].reshape(members * rows, HEAD_DIM)
                heads_d = da[c, :, :, head_cols].reshape(members * rows, HEAD_DIM)
                low = 3 * (c * per_group + g)
                minus_s = jnp.where((key_lane >= low) & (key_lane < low + 3), -1.0, 0.0)
                low = low + 3 * QH
                minus_d = jnp.where((key_lane >= low) & (key_lane < low + 3), -1.0, 0.0)
                s = lax.dot_general(jnp.concatenate([kt, minus_s.astype(BF)], 1),
                                    jnp.concatenate([heads_q, aux_all], 1), nt,
                                    preferred_element_type=F32)
                dp = lax.dot_general(jnp.concatenate([vt, minus_d.astype(BF)], 1),
                                     jnp.concatenate([heads_d, aux_all], 1), nt,
                                     preferred_element_type=F32)
                prob = jnp.exp2(s * (scale * math.log2(math.e)))
                dv = dv + jnp.dot(prob.astype(BF), heads_d, preferred_element_type=F32)
                ds = (prob * dp).astype(BF)
                dk = dk + jnp.dot(ds, heads_q, preferred_element_type=F32)
                acc[:, head_cols] += lax.dot_general(
                    ds, kt, (((0,), (0,)), ((), ())), preferred_element_type=F32)
            dks[c, side, at, :] = (dk * scale).astype(BF)
            dvs[c, side, at, :] = dv.astype(BF)
            return carry

        if first:
            acc[...] = jnp.zeros(acc.shape, F32)
        lax.fori_loop(0, tiles, one, 0)

    def finish(c):
        part[c] = (acc[...] * scale).reshape(na, nb, nd, rows, group).astype(BF)

    mid = group // 2
    left, right = pl.ds(0, mid), pl.ds(mid, mid)
    reduced = []

    def red(src, dst, to):
        n = len(reduced)
        copy = pltpu.make_async_remote_copy(
            src_ref=src, dst_ref=dst, send_sem=red_send.at[n], recv_sem=red_recv.at[n],
            device_id=place.device(to), device_id_type=MESH)
        copy.start()
        reduced.append(copy)
        return copy

    def stage1(c):
        stage = []
        for s in range(1, nd):
            to = place.other(2, s)
            stage.append(red(part.at[c, :, :, to[2], :, left], r1a.at[c, s - 1], to))
        for s in range(1, na):
            to = place.other(0, s)
            stage.append(red(part.at[c, to[0], :, :, :, right], r1b.at[c, s - 1], to))
        return stage

    def stage2(c, stage):
        for copy in stage:
            copy.wait_recv()
        for i in range(na):
            for j in range(nb):
                total = part[c, i, j, pd, :, left].astype(F32)
                for s in range(nd - 1):
                    total = total + r1a[c, s, i, j].astype(F32)
                t1a[c, i, j] = total.astype(BF)
        for j in range(nb):
            for i in range(nd):
                total = part[c, pa, j, i, :, right].astype(F32)
                for s in range(na - 1):
                    total = total + r1b[c, s, j, i].astype(F32)
                t1b[c, i, j] = total.astype(BF)
        stage = []
        for s in range(1, na):
            to = place.other(0, s)
            stage.append(red(t1a.at[c, to[0]], r2a.at[c, s - 1], to))
        for s in range(1, nd):
            to = place.other(2, s)
            stage.append(red(t1b.at[c, to[2]], r2b.at[c, s - 1], to))
        return stage

    def stage3(c, stage):
        for copy in stage:
            copy.wait_recv()
        for j in range(nb):
            total = t1a[c, pa, j].astype(F32)
            for s in range(na - 1):
                total = total + r2a[c, s, j].astype(F32)
            t2[c, j, :, left] = total.astype(BF)
            total = t1b[c, pd, j].astype(F32)
            for s in range(nd - 1):
                total = total + r2b[c, s, j].astype(F32)
            t2[c, j, :, right] = total.astype(BF)
        stage = []
        for s in range(1, nb):
            to = place.other(1, s)
            stage.append(red(t2.at[c, to[1]], r3.at[c, s - 1], to))
        return stage

    def last(c, stage):
        for copy in stage:
            copy.wait_recv()
        total = t2[c, pb].astype(F32)
        for s in range(nb - 1):
            total = total + r3[c, s].astype(F32)
        dq_out[:, pl.ds(c * group, group)] = total

    kv = []
    for c in range(KVH):
        attend(c, 1, True)
        kv.append(to_partner(dks.at[c, 1], kvr.at[c, 0]))
        kv.append(to_partner(dvs.at[c, 1], kvr.at[c, 1]))
        if c == 0:
            send_corner(("q1", "d1"))
        else:
            stage = stage2(0, stage)
        attend(c, 0, False)
        finish(c)
        if c == 0:
            stage = stage1(0)
            need_all(("q1", "d1"))
    ending = stage1(1)
    stage = stage3(0, stage)

    for copy in kv:
        copy.wait_recv()

    def add_part(n, carry):
        at = pl.ds(pl.multiple_of(n * chunk, chunk), chunk)
        for c in range(KVH):
            cols = pl.ds(c * HEAD_DIM, HEAD_DIM)
            for out, mine, where in ((dk_out, dks, 0), (dv_out, dvs, 1)):
                out[at, cols] = (mine[c, 0, at, :].astype(F32)
                                 + kvr[c, where, at, :].astype(F32)).astype(BF)
        return carry

    lax.fori_loop(0, keys // chunk, add_part, 0)
    ending = stage2(1, ending)
    last(0, stage)
    ending = stage3(1, ending)
    last(1, ending)
    for copy in started + partner_copies + reduced:
        copy.wait_send()


def local(dims, q, d, o, lse, k, v):
    na, nb, nd = dims
    members = na * nb * nd
    rows, width = q.shape
    keys, kw = k.shape
    group, mid = width // KVH, width // KVH // 2
    tile = min(512, keys)
    gathered, reduced = counts(dims)
    vmem = pl.BlockSpec(memory_space=pltpu.VMEM)
    ma, mb, md = max(na - 1, 1), max(nb - 1, 1), max(nd - 1, 1)
    sem = pltpu.SemaphoreType.DMA
    return pl.pallas_call(
        functools.partial(whole_kernel, dims, keys * members * 2, tile),
        name="whole",
        out_shape=(
            jax.ShapeDtypeStruct((rows, width), F32),
            jax.ShapeDtypeStruct((keys, kw), BF),
            jax.ShapeDtypeStruct((keys, kw), BF),
        ),
        in_specs=[vmem] * 6,
        out_specs=(vmem,) * 3,
        scratch_shapes=[
            pltpu.VMEM((KVH, members, rows, group), BF),
            pltpu.VMEM((KVH, members, rows, group), BF),
            pltpu.VMEM((members, rows + 16, HEAD_DIM), BF),
            pltpu.VMEM((members * rows, HEAD_DIM), BF),
            pltpu.VMEM((2, keys, kw), BF),
            pltpu.VMEM((2, keys, kw), BF),
            pltpu.VMEM((16, HEAD_DIM), F32),
            pltpu.VMEM((16, HEAD_DIM), F32),
            pltpu.VMEM((members * rows, group), F32),
            pltpu.VMEM((KVH, na, nb, nd, rows, group), BF),
            pltpu.VMEM((KVH, 2, keys, HEAD_DIM), BF),
            pltpu.VMEM((KVH, 2, keys, HEAD_DIM), BF),
            pltpu.VMEM((KVH, 2, keys, HEAD_DIM), BF),
            pltpu.VMEM((KVH, md, na, nb, rows, mid), BF),
            pltpu.VMEM((KVH, ma, nb, nd, rows, mid), BF),
            pltpu.VMEM((KVH, na, nb, rows, mid), BF),
            pltpu.VMEM((KVH, nd, nb, rows, mid), BF),
            pltpu.VMEM((KVH, ma, nb, rows, mid), BF),
            pltpu.VMEM((KVH, md, nb, rows, mid), BF),
            pltpu.VMEM((KVH, nb, rows, group), BF),
            pltpu.VMEM((KVH, mb, rows, group), BF),
            sem((gathered,)),
            sem((KVH, members)),
            sem((KVH, members)),
            sem((members,)),
            sem((3 + 2 * KVH,)),
            sem((3 + 2 * KVH,)),
            sem((reduced,)),
            sem((reduced,)),
        ],
        compiler_params=pltpu.CompilerParams(
            collective_id=0, has_side_effects=True, vmem_limit_bytes=60 * 1024 * 1024),
    )(q, d, o, lse, k, v)


def solution(mesh):
    dims = grid_of(mesh.shape["sa"], mesh.shape["sb"])
    spec = P(("sa", "sb"), None)
    return jax.shard_map(functools.partial(local, dims), mesh=mesh, in_specs=(spec,) * 6,
                         out_specs=(spec,) * 3, check_vma=False)
```

time: 446 us -> 74.2 us (0.17)
  waiting for transfers between devices: 149 us -> 0 us
  matrix products: 111 us -> 0 us
  blocking collectives: 108 us -> 0 us
  Pallas kernels: 0 us -> 67.7 us
  loops' own time: 36.7 us -> 0 us
  other arithmetic: 14.7 us -> 0 us
  between operations: 13.9 us -> 0.64 us
  local copies, waits for them, and re-layouts: 10.5 us -> 5.66 us
    dot_general x40 -> x0, matrix products: 111 us -> none  [the longest x8 29.1 us: one_head(): jnp.einsum('qd,kd->qk', head_queries, head_keys, preferred_element_type=j...]
    reduce_scatter x2 -> x0, waiting for transfers between devices: 89.6 us -> none  [the longest x1 59.4 us: local(): lax.psum_scatter(halfway, 'sb', scatter_dimension=1, tiled=True)]
    all_gather x1 -> x0, blocking collectives: 70.8 us -> none  [local(): shift_all = lax.all_gather(lse_shift, ('sa', 'sb'), axis=0, tiled=True)]
    pallas_call x0 -> x1, Pallas kernels: none -> 67.7 us  [local(): pl.pallas_call(functools.partial(whole_kernel, dims, keys * members * 2,...]
    all_gather x3 -> x0, waiting for transfers between devices: 57.5 us -> none  [the longest x1 48.5 us: local(): lax.all_gather(queries, ('sa', 'sb'), axis=0, tiled=True)]
    psum x1 -> x0, blocking collectives: 37.2 us -> none  [local(): lax.psum(jnp.sum(key_rows.astype(jnp.float32), axis=0), ('sa', 'sb'))]
    another operation x1 -> x0, loops' own time: 36.7 us -> none  [local(): lax.map(one_head, jnp.arange(QH, dtype=jnp.int32))]
    reduce_sum x3 -> x0, other arithmetic: 8.95 us -> none  [the longest x1 4.34 us: local(): value_heads.reshape(KVH, per_group, local_keys, HEAD_DIM).sum(axis=1)]
  transfers between devices with their start and end apart: 5 -> 0, of which waited for: 4 -> 0; matrix products, arithmetic and copies ran while one was open for 4% -> 0% of each run, Pallas kernels for 0% -> 0%
where the time goes in v2:
time: 74.2 us; the launch traced here: 74 us
  Pallas kernels  67.7 us (91%)
  local copies, waits for them, and re-layouts  5.66 us (8%)
    pallas_call x1, Pallas kernels, local(): pl.pallas_call(functools.partial(whole_kernel, dims, keys * members * 2,...  67.7 us
    unnamed x6, local copies, waits for them, and re-layouts  5.66 us

profile of v2, /device:TPU:0, one launch (start us, length us, event | category | flops | bytes accessed | tf_op | source)
XLA Modules:
  0.0 74.0 jit_solution(16219540101710137829)
XLA Ops:
  0.6 1.4 %copy.9.lse_ref = f32[32,8]{1,0:T(8,128)} copy(f32[32,8]{0,1:T(8,128)} %param.9) | data formatting | bytes 2048 | tf_op args[3]
  2.0 67.7 %whole.1 = (f32[32,1024]{1,0:T(8,128)}, bf16[1024,256]{1,0:T(8,128)(2,1)}, bf16[1024,256]{1,0:T(8,128)(2,1)}) custom-call(bf16[32,1024]{1,0:T(8,128)(2,1)} %q_ref.1, bf16[32,1024]{1,0:T(8,128)(2,1)} %d_ref.1, bf16[32,1024]{1,0:T(8,128)(2,1)} %o_ref.1, f32[32,8]{1,0:T(8,128)} %copy.9.lse_ref, bf16[1024,256]{1,0:T(8,128)(2,1)} %k_ref.1, bf16[1024,256]{1,0:T(8,128)(2,1)} %v_ref.1), custom_call_target="tpu_custom_call" | custom-call | tf_op jit(solution)/shard_map/whole/pallas_call | solution.py:425
  69.7 1.6 %copy.13 = f32[32,1024]{1,0:T(8,128)} copy(f32[32,1024]{1,0:T(8,128)} %get-tuple-element.6) | data formatting | bytes 262144
  71.3 0.0 copy-start
  71.3 1.9 %copy.14 = bf16[1024,256]{1,0:T(8,128)(2,1)} copy(bf16[1024,256]{1,0:T(8,128)(2,1)} %get-tuple-element.7) | data formatting | bytes 1048576
  73.2 0.0 copy-done
  73.2 0.8 %copy.15 = bf16[1024,256]{1,0:T(8,128)(2,1)} copy(bf16[1024,256]{1,0:T(8,128)(2,1)S(1)} %copy-done) | data formatting | bytes 1048576
Async XLA Ops:
  71.3 1.9 %copy-start = (bf16[1024,256]{1,0:T(8,128)(2,1)S(1)}, bf16[1024,256]{1,0:T(8,128)(2,1)}, u32[]{:S(2)}) copy-start(bf16[1024,256]{1,0:T(8,128)(2,1)} %get-tuple-element.8) | copy-start | bytes 1572868
